TPU v7x, 16 devices: a 4x2x1 block of a 4x4x8 slice. The times are simulated.
16 devices in a mesh: dp: 2 (over y, z), ep: 8 (over x, core).
Axes of the slice: x: 4, y: 2, z: 1, core: 2. Of those that a mesh axis runs over, the one named last changes fastest.
The devices are a block of a 4x4x8 slice.
Arguments:
- tokens: bfloat16 [2048, 2048], P(('dp', 'ep')), parts along dimension 0
- routes: int32 [2048, 8], P(('dp', 'ep')), parts along dimension 0
- w_router: bfloat16 [2048, 64], replicated
- w_one: bfloat16 [64, 2048, 1024], P('ep')
- w_three: bfloat16 [64, 2048, 1024], P('ep')
- w_two: bfloat16 [64, 1024, 2048], P('ep')
Outputs:
- output: bfloat16 [2048, 2048], P(('dp', 'ep')), parts along dimension 0
There are 2 independent parts. A program takes and returns all parts, laid end to end along the dimension named above; an argument that names none is the same for every part.
All inputs are finite; a program needn't handle non-finite values.
Results may differ from a plain program's by a relative error of at most 0.00817308.
Values are sent between devices in bfloat16 or wider.
A program may use at most 768 MiB of HBM per device.

v0:
```python
import jax
import jax.numpy as jnp
from jax import lax
from jax.sharding import PartitionSpec as P


def slot_capacity(num_tokens, top_k, num_experts):
    return 8 * ((3 * num_tokens * top_k + 16 * num_experts - 1) // (16 * num_experts))


def route_gates(tokens, routes, w_router):
    logits = jnp.dot(tokens, w_router, preferred_element_type=jnp.float32)
    return jax.nn.softmax(jnp.take_along_axis(logits, routes, axis=1), axis=-1)


def dispatch_plan(routes, num_experts, capacity):
    top_k = routes.shape[1]
    flat_routes = routes.reshape(-1)
    num_pairs = flat_routes.shape[0]
    sort_order = jnp.argsort(flat_routes, stable=True)
    counts = jax.ops.segment_sum(jnp.ones_like(flat_routes), flat_routes, num_segments=num_experts)
    starts = jnp.cumsum(counts) - counts
    slot_ids = starts[:, None] + jnp.arange(capacity, dtype=jnp.int32)[None, :]
    token_at = sort_order[jnp.minimum(slot_ids, num_pairs - 1)] // top_k
    pair_rank = jnp.zeros_like(sort_order).at[sort_order].set(jnp.arange(num_pairs, dtype=sort_order.dtype))
    pair_row = flat_routes * capacity + pair_rank - starts[flat_routes]
    return token_at, pair_row


def expert_mlp(rows, w_one, w_three, w_two):
    gate_pre = jnp.einsum('erd,edf->erf', rows, w_one, preferred_element_type=jnp.float32)
    up_pre = jnp.einsum('erd,edf->erf', rows, w_three, preferred_element_type=jnp.float32)
    hidden = (jax.nn.silu(gate_pre) * up_pre).astype(jnp.bfloat16)
    return jnp.einsum('erf,efd->erd', hidden, w_two, preferred_element_type=jnp.float32).astype(jnp.bfloat16)


def solution(mesh):
    group_size = mesh.shape['ep']
    row_spec = P(('dp', 'ep'), None)
    expert_spec = P('ep', None, None)

    def device_step(tokens, routes, w_router, w_one, w_three, w_two):
        num_tokens, d_model = tokens.shape
        top_k = routes.shape[1]
        num_experts = w_router.shape[1]
        local_experts = w_one.shape[0]
        capacity = slot_capacity(num_tokens, top_k, num_experts)
        gate_vals = route_gates(tokens, routes, w_router)
        token_at, pair_row = dispatch_plan(routes, num_experts, capacity)
        send_rows = tokens[token_at].reshape(num_experts, 1, capacity, d_model)
        recv_rows = lax.all_to_all(send_rows, 'ep', 0, 1, tiled=True)
        out_rows = expert_mlp(recv_rows.reshape(local_experts, group_size * capacity, d_model), w_one, w_three, w_two)
        back_rows = lax.all_to_all(out_rows.reshape(local_experts, group_size, capacity, d_model), 'ep', 1, 0, tiled=True)
        pair_out = back_rows.reshape(num_experts * capacity, d_model)[pair_row].reshape(num_tokens, top_k, d_model)
        return jnp.sum(gate_vals[:, :, None] * pair_out, axis=1).astype(jnp.bfloat16)

    return jax.shard_map(device_step, mesh=mesh, in_specs=(row_spec, row_spec, P(None, None), expert_spec, expert_spec, expert_spec), out_specs=row_spec, check_vma=False)
```

profile of v0, /device:TPU:112, one launch (start us, length us, event | category | flops | bytes accessed | tf_op | source)
XLA Modules:
  0.0 259.1 jit_solution(6473493746118275836)
XLA Ops:
  0.0 0.8 copy.34
  1.0 7.6 %scatter_custom_fusion = s32[64]{0:T(128)S(1)} fusion(s32[1024]{0:T(1024)S(1)} %reshape.205, s32[1024]{0:T(1024)S(1)} %broadcast.297, s32[]{:T(128)} %constant.17.clone.1), kind=kCustom, calls=%fused_computation.99 | custom fusion | flops 1024 | bytes 260 | tf_op jit(solution)/shard_map/scatter-add | solution.py:21
  8.9 4.4 %sort.17 = (s32[1024]{0:T(1024)}, s32[1024]{0:T(1024)S(1)}) sort(s32[1024]{0:T(1024)S(1)} %reshape.205, s32[1024]{0:T(1024)S(1)} %iota.13), dimensions={0}, to_apply=%region_2.3 | sort | flops 10240 | bytes 16384 | tf_op jit(solution)/shard_map/jit(argsort)/sort | solution.py:20
  13.4 5.9 %gather_fusion = s32[1536]{0:T(1024)S(1)} fusion(s32[1024]{0:T(1024)S(1)} %get-tuple-element.6, s32[2048]{0:T(1024)S(1)} %pad_clamp_fusion.1), kind=kCustom, calls=%fused_computation | custom fusion | bytes 18432 | tf_op jit(solution)/shard_map/gather | solution.py:24
  19.5 7.1 %gather_fusion.1 = bf16[1536,2048]{1,0:T(8,128)(2,1)} fusion(bf16[128,2048]{1,0:T(8,128)(2,1)S(1)} %copy-done, s32[2048]{0:T(1024)S(1)} %pad_clamp_fusion), kind=kCustom, calls=%fused_computation.1 | custom fusion | bytes 12589056 | tf_op jit(solution)/shard_map/gather | solution.py:50
  26.6 77.3 %all_to_all.30 = bf16[64,1,24,2048]{3,2,1,0:T(8,128)(2,1)S(1)} all-to-all(bf16[64,1,24,2048]{3,2,1,0:T(8,128)(2,1)} %bitcast.97), channel_id=1, replica_groups=mesh['dp'=2,'ep'=8] {'ep'}, dimensions={0} | all-to-all | bytes 12582912 | tf_op jit(solution)/shard_map/all_to_all | solution.py:51
  104.0 3.2 %copy.37 = bf16[8,8,1,24,2048]{4,3,1,0,2:T(8,128)(2,1)} copy(bf16[8,8,1,24,2048]{4,3,0,1,2:T(8,128)(2,1)S(1)} %bitcast.98) | data formatting | bytes 12582912 | tf_op jit(solution)/shard_map/all_to_all | solution.py:51
  107.2 18.3 %fusion.20 = f32[8,192,1024]{2,1,0:T(8,128)} fusion(bf16[8,192,2048]{2,1,0:T(8,128)(2,1)} %bitcast.99, bf16[8,2048,1024]{2,1,0:T(8,128)(2,1)} %param.9), kind=kOutput, calls=%fused_computation.108 | convolution fusion | flops 6442450944 | bytes 46137344 | tf_op jit(solution)/shard_map/erd,edf->erf/dot_general | solution.py:31
  125.5 30.3 %convolution_convert_fusion = bf16[8,192,2048]{2,1,0:T(8,128)(2,1)} fusion(bf16[8,1024,2048]{2,1,0:T(8,128)(2,1)} %param.11, f32[8,192,1024]{2,1,0:T(8,128)} %fusion.20, bf16[8,192,2048]{2,1,0:T(8,128)(2,1)} %bitcast.100, bf16[8,2048,1024]{2,1,0:T(8,128)(2,1)} %param.10), kind=kOutput, calls=%fused_computation.9 | convolution fusion | flops 12897484800 | bytes 85983232 | tf_op jit(solution)/shard_map/erf,efd->erd/dot_general | solution.py:34
  155.8 6.6 %copy.38 = bf16[8,8,24,2048]{3,2,0,1:T(8,128)(2,1)} copy(bf16[8,8,24,2048]{3,2,1,0:T(8,128)(2,1)} %bitcast.101) | data formatting | bytes 12582912 | tf_op jit(solution)/shard_map/reshape | solution.py:53
  162.4 5.2 %all-to-all-start.1 = ((bf16[8,8,24,2048]{3,2,0,1:T(8,128)(2,1)}), bf16[8,8,24,2048]{3,2,0,1:T(8,128)(2,1)}, u32[]{:S(2)}, u32[]{:S(2)}) async-start(bf16[8,8,24,2048]{3,2,0,1:T(8,128)(2,1)} %copy.38), calls=%async_computation.1 | async-start | bytes 12582912 | tf_op jit(solution)/shard_map/all_to_all | solution.py:53
  168.0 0.3 fusion.19
  168.3 7.0 %gather_fusion.3 = f32[1024]{0:T(1024)S(1)} fusion(f32[128,64]{0,1:T(8,128)S(1)} %fusion.19, s32[1024]{0:T(1024)S(1)} %reshape.308), kind=kCustom, calls=%fused_computation.3 | custom fusion | bytes 16384 | tf_op jit(solution)/shard_map/jit(take_along_axis)/gather | solution.py:13
  175.6 4.3 %scatter_custom_fusion.1 = s32[1024]{0:T(1024)S(1)} fusion(s32[1024]{0:T(1024)S(1)} %compare_select_fusion.10, s32[1024]{0:T(1024)S(1)} %iota.14, s32[]{:T(128)} %constant.17.clone.1), kind=kCustom, calls=%fused_computation.97 | custom fusion | bytes 4100 | tf_op jit(solution)/shard_map/scatter | solution.py:25
  180.0 0.7 fusion.18
  180.6 0.7 fusion.17
  181.4 0.7 fusion.15
  182.1 0.7 fusion.16
  182.8 4.5 %compare_select_fusion.3 = (s32[1024,1]{0,1:T(1,128)S(1)}, s32[1024,1]{0,1:T(1,128)S(1)}) fusion(s32[]{:T(128)} %bitcast.68, s32[]{:T(128)} %bitcast.69, s32[]{:T(128)} %bitcast.70, s32[]{:T(128)} %bitcast.71, s32[]{:T(128)} %bitcast.72, s32[]{:T(128)} %bitcast.74, s32[]{:T(128)} %bitcast.73, s32[1024,1]{0,1:T(1,128)S(1)} %broadcast_in_dim_reshape.3), kind=kLoop, calls=%fused_computation.79 | loop fusion | flops 15360 | bytes 12316 | tf_op jit(solution)/shard_map/gather | solution.py:26
  187.3 0.7 compare_reduce_fusion.56
  188.0 35.3 %fusion.6 = s32[1024]{0:T(1024)S(1)} fusion(pred[1024]{0:T(1024)(128)(4,1)S(1)} %get-tuple-element.63, pred[1024]{0:T(1024)(128)(4,1)S(1)} %get-tuple-element.62, pred[1024]{0:T(1024)(128)(4,1)S(1)} %get-tuple-element.61, pred[1024]{0:T(1024)(128)(4,1)S(1)} %get-tuple-element.60, pred[1024]{0:T(1024)(128)(4,1)S(1)} %get-tuple-element.59, ...), kind=kLoop, calls=%fused_computation.90 | loop fusion | flops 65536 | bytes 74980 | tf_op jit(solution)/shard_map/gather | solution.py:54
  223.3 16.0 %all-to-all-done.1 = bf16[8,8,24,2048]{3,2,0,1:T(8,128)(2,1)} async-done(((bf16[8,8,24,2048]{3,2,0,1:T(8,128)(2,1)}), bf16[8,8,24,2048]{3,2,0,1:T(8,128)(2,1)}, u32[]{:S(2)}, u32[]{:S(2)}) %all-to-all-start.1) | async-done | bytes 6291488 | tf_op jit(solution)/shard_map/all_to_all | solution.py:53
  239.4 12.4 %gather_fusion.2 = bf16[1024,2048]{1,0:T(8,128)(2,1)} fusion(bf16[1536,2048]{1,0:T(8,128)(2,1)} %bitcast.10, s32[1024]{0:T(1024)S(1)} %fusion.6), kind=kCustom, calls=%fused_computation.2 | custom fusion | bytes 8392704 | tf_op jit(solution)/shard_map/gather | solution.py:54
  251.8 7.3 %fusion = bf16[128,2048]{1,0:T(8,128)(2,1)} fusion(bf16[1024,2048]{1,0:T(8,128)(2,1)} %gather_fusion.2, f32[128,8]{1,0:T(8,128)S(1)} %copy.33), kind=kLoop, calls=%fused_computation.7 | loop fusion | flops 6029312 | bytes 4722688 | tf_op jit(solution)/shard_map/reduce_sum | solution.py:55
  (32 shorter events, 1.4 us)
Async XLA Ops:
  0.0 19.5 %copy-start = (bf16[128,2048]{1,0:T(8,128)(2,1)S(1)}, bf16[128,2048]{1,0:T(8,128)(2,1)}, u32[]{:S(2)}) copy-start(bf16[128,2048]{1,0:T(8,128)(2,1)} %param.6) | copy-start | bytes 1572868
  162.4 5.3 %copy-start.2 = (s32[128,8]{0,1:T(8,128)S(1)}, s32[128,8]{0,1:T(8,128)}, u32[]{:S(2)}) copy-start(s32[128,8]{0,1:T(8,128)} %param.7) | copy-start | bytes 12292
  162.4 5.6 %copy-start.1 = (bf16[2048,64]{0,1:T(8,128)(2,1)S(1)}, bf16[2048,64]{0,1:T(8,128)(2,1)}, u32[]{:S(2)}) copy-start(bf16[2048,64]{0,1:T(8,128)(2,1)} %param.8) | copy-start | bytes 786436
  162.4 77.0 %all-to-all-start.1 = ((bf16[8,8,24,2048]{3,2,0,1:T(8,128)(2,1)}), bf16[8,8,24,2048]{3,2,0,1:T(8,128)(2,1)}, u32[]{:S(2)}, u32[]{:S(2)}) async-start(bf16[8,8,24,2048]{3,2,0,1:T(8,128)(2,1)} %copy.38), calls=%async_computation.1 | async-start | bytes 12582912 | tf_op jit(solution)/shard_map/all_to_all | solution.py:53
where the time goes:
time: 260 us; the launch traced here: 259 us
  blocking collectives  77.3 us (30%)
  other arithmetic  60.2 us (23%)
  local copies, waits for them, and re-layouts  51.1 us (20%)
  matrix products  48.9 us (19%)
  waiting for transfers between devices  16 us (6%)
  starting transfers between devices  5.23 us (2%)
    all_to_all x1, blocking collectives, device_step(): recv_rows = lax.all_to_all(send_rows, 'ep', 0, 1, tiled=True)  77.3 us
    gather x1, other arithmetic, device_step(): back_rows.reshape(num_experts * capacity, d_model)[pair_row]  35.3 us
    dot_general x1, matrix products, expert_mlp(): jnp.einsum('erf,efd->erd', hidden, w_two, preferred_element_type=jnp.floa...  30.3 us
    dot_general x1, matrix products, expert_mlp(): jnp.einsum('erd,edf->erf', rows, w_one, preferred_element_type=jnp.float32)  18.3 us
    all_to_all x1, waiting for transfers between devices, device_step(): lax.all_to_all(out_rows.reshape(local_experts, group_size, capacity, d_mo...  16 us
    gather x1, local copies, waits for them, and re-layouts, device_step(): back_rows.reshape(num_experts * capacity, d_model)[pair_row]  12.4 us
    scatter-add x1, other arithmetic, dispatch_plan(): jax.ops.segment_sum(jnp.ones_like(flat_routes), flat_routes, num_segments...  7.61 us
    gather x5, local copies, waits for them, and re-layouts, route_gates(): return jax.nn.softmax(jnp.take_along_axis(logits, routes, axis=1), axis=-1)  7.34 us
  transfers between devices with their start and end apart: 1, of which 1 were waited for; matrix products, arithmetic and copies ran while one was open for 21% of the time, Pallas kernels for 0%

commit v1 on v0

v1 whole, which is shorter than its diff:
```python
import functools

import jax
import jax.numpy as jnp
from jax import lax
from jax.experimental import pallas as pl
from jax.experimental.pallas import tpu as pltpu
from jax.sharding import PartitionSpec as P

MESH = pl.DeviceIdType.MESH
F32 = jnp.float32
BF16 = jnp.bfloat16

IN_CHUNKS = 4
OUT_CHUNKS = 8
W_SLOTS = 8
OWN_SLOTS = 4
UNROLL_IN = 2
UNROLL_OUT = 2


def slot_capacity(num_tokens, top_k, num_experts):
    return 8 * ((3 * num_tokens * top_k + 16 * num_experts - 1) // (16 * num_experts))


def moe_kernel(
    cap, tokens, routes, w_router, w_one, w_three, w_two, out,
    xs, us, acc_a, acc_b, hid, w1_buf, w3_buf, w2_buf, o_buf, pick, gate_mat,
    s_loc, g_loc, s_all, g_all, own, p_send, p_recv, h_recv, f_recv,
    tok_sem, w1_sem, w3_sem, w2_sem, ag_send, ag_recv, s_send, s_recv, g_send, g_recv,
    ps_sem, pr_sem, hs_sem, hr_sem, fs_sem, fr_sem,
):
    num_tokens, d_model = tokens.shape
    top_k = routes.shape[1]
    num_experts = w_router.shape[1]
    local_experts = w_one.shape[0]
    num_dev = num_experts // local_experts
    num_chips = num_dev // 2
    kc = d_model // IN_CHUNKS
    nw = d_model // OUT_CHUNKS
    rows = num_dev * cap
    slots = local_experts * cap
    half = num_tokens // 2

    me = lax.axis_index("ep")
    chip = me // 2
    core = lax.rem(me, 2)

    def at_chip(k):
        return lax.rem(chip + k, num_chips)

    right = at_chip(1) * 2 + core
    left = at_chip(num_chips - 1) * 2 + core
    opp = at_chip(2) * 2 + core
    partner = chip * 2 + 1 - core

    def w_copies(step):
        i = step // local_experts
        e = lax.rem(step, local_experts)
        slot = lax.rem(step, W_SLOTS)
        rng = pl.ds(pl.multiple_of(i * kc, kc), kc)
        return (
            pltpu.make_async_copy(w_one.at[e, rng, :], w1_buf.at[slot], w1_sem.at[slot]),
            pltpu.make_async_copy(w_three.at[e, rng, :], w3_buf.at[slot], w3_sem.at[slot]),
        )

    def w_start(step):
        for copy in w_copies(step):
            copy.start()

    def w2_copy(n):
        return pltpu.make_async_copy(
            w_two.at[:, :, pl.ds(n * nw, nw)], w2_buf.at[n % 2], w2_sem.at[n % 2]
        )

    def tok_copy(i):
        return pltpu.make_async_copy(
            tokens.at[:, pl.ds(i * kc, kc)], xs.at[i, me], tok_sem.at[i]
        )

    for i in range(IN_CHUNKS):
        tok_copy(i).start()
    for step in range(W_SLOTS):
        w_start(jnp.int32(step))

    barrier = pltpu.get_barrier_semaphore()
    for k in range(1, num_dev):
        pl.semaphore_signal(
            barrier, inc=1, device_id={"ep": lax.rem(me + k, num_dev)}, device_id_type=MESH
        )

    expert_id = lax.broadcasted_iota(jnp.int32, (num_tokens, num_experts), 1)
    member = jnp.zeros((num_tokens, num_experts), F32)
    for j in range(top_k):
        member = member + jnp.where(routes[:, j : j + 1] == expert_id, 1.0, 0.0)
    row_id = lax.broadcasted_iota(jnp.int32, (num_tokens, num_tokens), 0)
    col_id = lax.broadcasted_iota(jnp.int32, (num_tokens, num_tokens), 1)
    before = jnp.where(col_id < row_id, 1.0, 0.0).astype(BF16)
    rank = jnp.dot(before, member.astype(BF16), preferred_element_type=F32)
    slot_of = jnp.where(member > 0.5, rank, -1.0)
    s_loc[...] = slot_of.T.reshape(num_dev, local_experts, num_tokens)
    s_all[me] = s_loc[me]

    pl.semaphore_wait(barrier, num_dev - 1)

    def plan_copy(k, src, dst, send, recv):
        peer = lax.rem(me + k, num_dev)
        return pltpu.make_async_remote_copy(
            src_ref=src.at[peer], dst_ref=dst.at[me], send_sem=send.at[k - 1],
            recv_sem=recv.at[k - 1], device_id={"ep": peer}, device_id_type=MESH,
        )

    for k in range(1, num_dev):
        plan_copy(k, s_loc, s_all, s_send, s_recv).start()

    low, high, full = pl.ds(0, half), pl.ds(half, half), pl.ds(0, num_tokens)
    ag_table = (
        (me, full, right), (me, full, left), (me, full, partner),
        (left, low, right), (right, high, left),
        (left, full, partner), (right, full, partner),
        (opp, low, partner), (opp, high, partner),
    )

    def ag(i, kind):
        block, rng, dest = ag_table[kind]
        ref = xs.at[i, block, rng, :]
        return pltpu.make_async_remote_copy(
            src_ref=ref, dst_ref=ref, send_sem=ag_send.at[i, kind],
            recv_sem=ag_recv.at[i, kind], device_id={"ep": dest}, device_id_type=MESH,
        )

    def ag_own(i):
        if i < IN_CHUNKS:
            for kind in (0, 1, 2):
                ag(i, kind).start()

    def ag_stage1(i):
        if i < IN_CHUNKS:
            ag(i, 0).wait_recv()
            ag(i, 3).start()
            ag(i, 5).start()
            ag(i, 1).wait_recv()
            ag(i, 4).start()
            ag(i, 6).start()
            ag_own(i + 2)

    def ag_stage2(i):
        if i < IN_CHUNKS:
            ag(i, 3).wait_recv()
            ag(i, 7).start()
            ag(i, 4).wait_recv()
            ag(i, 8).start()

    def ag_stage3(i):
        if i < IN_CHUNKS:
            for kind in (2, 5, 6, 7, 8):
                ag(i, kind).wait_recv()

    for i in range(IN_CHUNKS):
        tok_copy(i).wait()
    ag_own(0)
    ag_own(1)

    logits = jnp.dot(xs[0, me], w_router[0:kc, :], preferred_element_type=F32)
    for i in range(1, IN_CHUNKS):
        logits = logits + jnp.dot(
            xs[i, me], w_router[i * kc : (i + 1) * kc, :], preferred_element_type=F32
        )
    chosen = member > 0.5
    peak = jnp.max(jnp.where(chosen, logits, -jnp.inf), axis=1, keepdims=True)
    powers = jnp.where(chosen, jnp.exp(jnp.where(chosen, logits - peak, 0.0)), 0.0)
    gates = powers / jnp.sum(powers, axis=1, keepdims=True)
    g_loc[...] = gates.T.reshape(num_dev, local_experts, num_tokens)
    g_all[me] = g_loc[me]
    for k in range(1, num_dev):
        plan_copy(k, g_loc, g_all, g_send, g_recv).start()

    slot_id = lax.broadcasted_iota(jnp.int32, (cap, num_tokens), 0).astype(F32)
    for k in range(1, num_dev):
        plan_copy(k, s_loc, s_all, s_send, s_recv).wait_recv()

    def build_pick(q, carry):
        parts = [
            jnp.where(s_all[q, e : e + 1, :] == slot_id, 1.0, 0.0) for e in range(local_experts)
        ]
        pick[q] = jnp.concatenate(parts, axis=0).astype(BF16)
        return carry

    lax.fori_loop(0, num_dev, build_pick, 0)

    def build_gates(q, carry):
        parts = [
            jnp.where(s_all[q, e : e + 1, :] == slot_id, g_all[q, e : e + 1, :], 0.0)
            for e in range(local_experts)
        ]
        mat = jnp.concatenate(parts, axis=0).T
        top = mat.astype(BF16)
        rest = mat - top.astype(F32)
        mid = rest.astype(BF16)
        gate_mat[q, 0] = top
        gate_mat[q, 1] = mid
        gate_mat[q, 2] = (rest - mid.astype(F32)).astype(BF16)
        return carry

    def gather(i):
        def one_source(q, carry):
            picked = jnp.dot(pick[q], xs[i, q], preferred_element_type=F32)
            base = pl.multiple_of(q * cap, 8)
            us[:, pl.ds(base, cap), :] = picked.reshape(local_experts, cap, kc)
            return carry

        lax.fori_loop(0, num_dev, one_source, 0, unroll=2)

    def experts(i, lo, hi):
        def one_expert(e):
            step = i * local_experts + e
            slot = lax.rem(step, W_SLOTS)
            c1, c3 = w_copies(step)
            u = us[e].astype(BF16)
            c1.wait()
            a = jnp.dot(u, w1_buf[slot], preferred_element_type=F32)
            if i > 0:
                a = a + acc_a[e]
            c3.wait()
            b = jnp.dot(u, w3_buf[slot], preferred_element_type=F32)
            if i > 0:
                b = b + acc_b[e]
            if i < IN_CHUNKS - 1:
                acc_a[e] = a
                acc_b[e] = b
            else:
                hid[e] = (jax.nn.silu(a) * b).astype(BF16)
            if (i + 1) * local_experts <= IN_CHUNKS * local_experts - W_SLOTS:
                w_start(step + W_SLOTS)

        def body(t, carry):
            for r in range(UNROLL_IN):
                one_expert(lo + t * UNROLL_IN + r)
            return carry

        lax.fori_loop(0, (hi - lo) // UNROLL_IN, body, 0)

    ag_stage1(0)
    ag_stage2(0)
    ag_stage3(0)
    mid_expert = local_experts // 2
    for i in range(IN_CHUNKS):
        gather(i)
        if i == IN_CHUNKS - 1:
            w2_copy(0).start()
            w2_copy(1).start()
        experts(i, 0, mid_expert)
        ag_stage1(i + 1)
        if i == 1:
            for k in range(1, num_dev):
                plan_copy(k, g_loc, g_all, g_send, g_recv).wait_recv()
            lax.fori_loop(0, num_dev, build_gates, 0)
        experts(i, mid_expert, local_experts)
        ag_stage2(i + 1)
        ag_stage3(i + 1)

    def partial(q):
        base = pl.multiple_of(q * cap, 8)
        o_rows = o_buf[:, pl.ds(base, cap), :].reshape(slots, nw).astype(BF16)
        total = jnp.dot(gate_mat[q, 2], o_rows, preferred_element_type=F32)
        total = total + jnp.dot(gate_mat[q, 1], o_rows, preferred_element_type=F32)
        return total + jnp.dot(gate_mat[q, 0], o_rows, preferred_element_type=F32)

    def p_copy(n):
        return pltpu.make_async_remote_copy(
            src_ref=p_send.at[n % 2], dst_ref=p_recv.at[n], send_sem=ps_sem.at[n],
            recv_sem=pr_sem.at[n], device_id={"ep": partner}, device_id_type=MESH,
        )

    def h_copy(n, d):
        return pltpu.make_async_remote_copy(
            src_ref=own.at[n % OWN_SLOTS, 2, low if d == 0 else high, :],
            dst_ref=h_recv.at[n, d], send_sem=hs_sem.at[n, d], recv_sem=hr_sem.at[n, d],
            device_id={"ep": right if d == 0 else left}, device_id_type=MESH,
        )

    def f_copy(n, d):
        return pltpu.make_async_remote_copy(
            src_ref=own.at[n % OWN_SLOTS, 1 if d == 0 else 3],
            dst_ref=f_recv.at[n, d], send_sem=fs_sem.at[n, d], recv_sem=fr_sem.at[n, d],
            device_id={"ep": right if d == 0 else left}, device_id_type=MESH,
        )

    def produce(n):
        if n >= 2:
            p_copy(n - 2).wait_send()
        if n >= OWN_SLOTS:
            for d in (0, 1):
                h_copy(n - OWN_SLOTS, d).wait_send()
                f_copy(n - OWN_SLOTS, d).wait_send()
        w2_copy(n).wait()

        def body(t, carry):
            for r in range(UNROLL_OUT):
                e = t * UNROLL_OUT + r
                o_buf[e] = jnp.dot(hid[e], w2_buf[n % 2, e], preferred_element_type=F32)
            return carry

        lax.fori_loop(0, local_experts // UNROLL_OUT, body, 0)
        if n + 2 < OUT_CHUNKS:
            w2_copy(n + 2).start()

        def for_partner(k, carry):
            p_send[n % 2, k] = partial(at_chip(k) * 2 + 1 - core)
            return carry

        def for_own(k, carry):
            own[n % OWN_SLOTS, k] = partial(at_chip(k) * 2 + core)
            return carry

        lax.fori_loop(0, num_chips, for_partner, 0)
        p_copy(n).start()
        lax.fori_loop(0, num_chips, for_own, 0)

    def send_halves(n):
        s = n % OWN_SLOTS
        p_copy(n).wait_recv()
        own[s, 2] = own[s, 2] + p_recv[n, 2]
        for d in (0, 1):
            h_copy(n, d).start()
        for k in (0, 1, 3):
            own[s, k] = own[s, k] + p_recv[n, k]

    def send_full(n):
        s = n % OWN_SLOTS
        for d, k, rng in ((0, 1, low), (1, 3, high)):
            h_copy(n, d).wait_recv()
            own[s, k, rng, :] = own[s, k, rng, :] + h_recv[n, d]
            f_copy(n, d).start()

    def finish(n):
        s = n % OWN_SLOTS
        for d in (0, 1):
            f_copy(n, d).wait_recv()
        out[:, n * nw : (n + 1) * nw] = (own[s, 0] + (f_recv[n, 0] + f_recv[n, 1])).astype(BF16)

    for n in range(OUT_CHUNKS + 2):
        if n < OUT_CHUNKS:
            produce(n)
            send_halves(n)
        if 1 <= n <= OUT_CHUNKS:
            send_full(n - 1)
        if n >= 2:
            finish(n - 2)

    for k in range(1, num_dev):
        plan_copy(k, s_loc, s_all, s_send, s_recv).wait_send()
        plan_copy(k, g_loc, g_all, g_send, g_recv).wait_send()
    for i in range(IN_CHUNKS):
        for kind in range(len(ag_table)):
            ag(i, kind).wait_send()
    for n in range(OUT_CHUNKS - 2, OUT_CHUNKS):
        p_copy(n).wait_send()
    for n in range(OUT_CHUNKS - OWN_SLOTS, OUT_CHUNKS):
        for d in (0, 1):
            h_copy(n, d).wait_send()
            f_copy(n, d).wait_send()


def solution(mesh):
    num_dev = mesh.shape["ep"]
    row_spec = P(("dp", "ep"), None)
    expert_spec = P("ep", None, None)

    def device_step(tokens, routes, w_router, w_one, w_three, w_two):
        num_tokens, d_model = tokens.shape
        num_experts = w_router.shape[1]
        local_experts, _, d_expert = w_one.shape
        cap = slot_capacity(num_tokens, routes.shape[1], num_experts)
        rows, slots = num_dev * cap, local_experts * cap
        kc, nw = d_model // IN_CHUNKS, d_model // OUT_CHUNKS
        chips, half = num_dev // 2, num_tokens // 2
        dma = pltpu.SemaphoreType.DMA
        any_spec = pl.BlockSpec(memory_space=pl.ANY)
        vmem_spec = pl.BlockSpec(memory_space=pltpu.VMEM)
        return pl.pallas_call(
            functools.partial(moe_kernel, cap),
            out_shape=jax.ShapeDtypeStruct((num_tokens, d_model), BF16),
            in_specs=[any_spec, vmem_spec, vmem_spec, any_spec, any_spec, any_spec],
            out_specs=vmem_spec,
            scratch_shapes=[
                pltpu.VMEM((IN_CHUNKS, num_dev, num_tokens, kc), BF16),
                pltpu.VMEM((local_experts, rows, kc), F32),
                pltpu.VMEM((local_experts, rows, d_expert), F32),
                pltpu.VMEM((local_experts, rows, d_expert), F32),
                pltpu.VMEM((local_experts, rows, d_expert), BF16),
                pltpu.VMEM((W_SLOTS, kc, d_expert), BF16),
                pltpu.VMEM((W_SLOTS, kc, d_expert), BF16),
                pltpu.VMEM((2, local_experts, d_expert, nw), BF16),
                pltpu.VMEM((local_experts, rows, nw), F32),
                pltpu.VMEM((num_dev, slots, num_tokens), BF16),
                pltpu.VMEM((num_dev, 3, num_tokens, slots), BF16),
                pltpu.VMEM((num_dev, local_experts, num_tokens), F32),
                pltpu.VMEM((num_dev, local_experts, num_tokens), F32),
                pltpu.VMEM((num_dev, local_experts, num_tokens), F32),
                pltpu.VMEM((num_dev, local_experts, num_tokens), F32),
                pltpu.VMEM((OWN_SLOTS, chips, num_tokens, nw), F32),
                pltpu.VMEM((2, chips, num_tokens, nw), F32),
                pltpu.VMEM((OUT_CHUNKS, chips, num_tokens, nw), F32),
                pltpu.VMEM((OUT_CHUNKS, 2, half, nw), F32),
                pltpu.VMEM((OUT_CHUNKS, 2, num_tokens, nw), F32),
                dma((IN_CHUNKS,)), dma((W_SLOTS,)), dma((W_SLOTS,)), dma((2,)),
                dma((IN_CHUNKS, 9)), dma((IN_CHUNKS, 9)),
                dma((num_dev - 1,)), dma((num_dev - 1,)), dma((num_dev - 1,)), dma((num_dev - 1,)),
                dma((OUT_CHUNKS,)), dma((OUT_CHUNKS,)),
                dma((OUT_CHUNKS, 2)), dma((OUT_CHUNKS, 2)),
                dma((OUT_CHUNKS, 2)), dma((OUT_CHUNKS, 2)),
            ],
            compiler_params=pltpu.CompilerParams(
                collective_id=0, has_side_effects=True, vmem_limit_bytes=67_000_000
            ),
            name="moe_step",
        )(tokens, routes, w_router, w_one, w_three, w_two)

    return jax.shard_map(
        device_step, mesh=mesh,
        in_specs=(row_spec, row_spec, P(None, None), expert_spec, expert_spec, expert_spec),
        out_specs=row_spec, check_vma=False,
    )
```

time: 260 us -> 114 us (0.44)
  Pallas kernels: 0 us -> 108 us
  blocking collectives: 77.3 us -> 0 us
  other arithmetic: 60.2 us -> 0 us
  matrix products: 48.9 us -> 0 us
  local copies, waits for them, and re-layouts: 51.1 us -> 5.24 us
  waiting for transfers between devices: 16 us -> 0 us
  starting transfers between devices: 5.23 us -> 0 us
    pallas_call x0 -> x1, Pallas kernels: none -> 108 us  [device_step(): pl.pallas_call(functools.partial(moe_kernel, cap), out_shape=jax.ShapeDty...]
    all_to_all x1 -> x0, blocking collectives: 77.3 us -> none  [device_step(): recv_rows = lax.all_to_all(send_rows, 'ep', 0, 1, tiled=True)]
    dot_general x3 -> x0, matrix products: 48.9 us -> none  [the longest x1 30.3 us: expert_mlp(): jnp.einsum('erf,efd->erd', hidden, w_two, preferred_element_type=jnp.floa...]
    gather x6 -> x0, other arithmetic: 40.5 us -> none  [the longest x1 35.3 us: device_step(): back_rows.reshape(num_experts * capacity, d_model)[pair_row]]
    gather x13 -> x0, local copies, waits for them, and re-layouts: 35.6 us -> none  [the longest x1 12.4 us: device_step(): back_rows.reshape(num_experts * capacity, d_model)[pair_row]]
    all_to_all x1 -> x0, waiting for transfers between devices: 16 us -> none  [device_step(): lax.all_to_all(out_rows.reshape(local_experts, group_size, capacity, d_mo...]
    scatter-add x1 -> x0, other arithmetic: 7.61 us -> none  [dispatch_plan(): jax.ops.segment_sum(jnp.ones_like(flat_routes), flat_routes, num_segments...]
    reduce_sum x2 -> x0, other arithmetic: 7.35 us -> none  [the longest x1 7.33 us: device_step(): jnp.sum(gate_vals[:, :, None] * pair_out, axis=1).astype(jnp.bfloat16)]
  transfers between devices with their start and end apart: 1 -> 0, of which waited for: 1 -> 0; matrix products, arithmetic and copies ran while one was open for 21% -> 0% of each run, Pallas kernels for 0% -> 0%
where the time goes in v1:
time: 114 us; the launch traced here: 113 us
  Pallas kernels  108 us (95%)
  local copies, waits for them, and re-layouts  5.24 us (5%)
    pallas_call x1, Pallas kernels, device_step(): pl.pallas_call(functools.partial(moe_kernel, cap), out_shape=jax.ShapeDty...  108 us
    unnamed x3, local copies, waits for them, and re-layouts  5.24 us

profile of v1, /device:TPU:112, one launch (start us, length us, event | category | flops | bytes accessed | tf_op | source)
XLA Modules:
  0.0 113.5 jit_solution(10756667928733309181)
XLA Ops:
  0.0 1.4 %copy.7.routes = s32[128,8]{1,0:T(8,128)} copy(s32[128,8]{0,1:T(8,128)} %param.7) | data formatting | bytes 8192 | tf_op args[1]
  1.4 2.0 %copy.8.w_router = bf16[2048,64]{1,0:T(8,128)(2,1)} copy(bf16[2048,64]{0,1:T(8,128)(2,1)} %param.8) | data formatting | bytes 524288 | tf_op args[2]
  3.4 108.2 %moe_step.1 = bf16[128,2048]{1,0:T(8,128)(2,1)} custom-call(bf16[128,2048]{1,0:T(8,128)(2,1)} %tokens.1, s32[128,8]{1,0:T(8,128)} %copy.7.routes, bf16[2048,64]{1,0:T(8,128)(2,1)} %copy.8.w_router, bf16[8,2048,1024]{2,1,0:T(8,128)(2,1)} %w_one.1, bf16[8,2048,1024]{2,1,0:T(8,128)(2,1)} %w_three.1, bf16[8,1024,2048]{2,1,0:T(8,128)(2,1)} %w_two.1), custom_call_target="tpu_custom_call" | custom-call | tf_op jit(solution)/shard_map/moe_step/pallas_call | solution.py:381
  111.6 1.9 %copy.10 = bf16[128,2048]{1,0:T(8,128)(2,1)} copy(bf16[128,2048]{1,0:T(8,128)(2,1)} %moe_step.1) | data formatting | bytes 1048576

commit v2 on v0

v2 whole, which is shorter than its diff:
```python
import functools

import jax
import jax.numpy as jnp
from jax import lax
from jax.experimental import pallas as pl
from jax.experimental.pallas import tpu as pltpu
from jax.sharding import PartitionSpec as P

MESH = pl.DeviceIdType.MESH
F32 = jnp.float32
BF16 = jnp.bfloat16

IN_SPLIT = (1, 2, 2, 2, 1)
OUT_SPLIT = (2, 2, 2, 2, 2, 2, 2, 2)
RING = 24
OWN_SLOTS = 4
FIN_LAG = 3
COLS = 256
EXP_GROUP = 4
GATHER_UNROLL = 4


def chunk_list(parts, total):
    unit = total // sum(parts)
    chunks, at = [], 0
    for part in parts:
        chunks.append((at, part * unit))
        at += part * unit
    return chunks


def slot_capacity(num_tokens, top_k, num_experts):
    return 8 * ((3 * num_tokens * top_k + 16 * num_experts - 1) // (16 * num_experts))


def loop(count, body, unroll):
    if unroll >= count:
        for t in range(count):
            body(t)
        return

    def step(t, carry):
        for r in range(unroll):
            body(t * unroll + r)
        return carry

    lax.fori_loop(0, count // unroll, step, 0)


def moe_kernel(
    cap, tokens, routes, w_router, w_one, w_three, w_two, out,
    xs, us, acc_a, acc_b, hid, pool, y_buf, pick, gate_mat,
    s_loc, g_loc, s_all, g_all, own, p_send, p_recv, h_recv, f_recv,
    tok_sem, in_sem, out_sem, ag_send, ag_recv, s_send, s_recv, g_send, g_recv,
    ps_sem, pr_sem, rs_send, hr_sem, fr_sem, y_sem,
):
    num_tokens, d_model = tokens.shape
    top_k = routes.shape[0]
    num_experts = w_router.shape[0]
    local_experts = w_one.shape[0]
    d_expert = w_one.shape[2]
    num_dev = num_experts // local_experts
    num_chips = num_dev // 2
    ins = chunk_list(IN_SPLIT, d_model)
    outs = chunk_list(OUT_SPLIT, d_model)
    num_in, num_out = len(ins), len(outs)
    unit = d_model // sum(IN_SPLIT)
    rows = num_dev * cap
    slots = local_experts * cap
    half = num_tokens // 2

    me = lax.axis_index("ep")
    chip = me // 2
    core = lax.rem(me, 2)

    def at_chip(k):
        return lax.rem(chip + k, num_chips)

    right = at_chip(1) * 2 + core
    left = at_chip(num_chips - 1) * 2 + core
    opp = at_chip(2) * 2 + core
    partner = chip * 2 + 1 - core

    tiles = d_expert // COLS
    unit_rows = 2 * tiles * unit
    pieces, in_at, out_at, at = [], {}, {}, 0
    for i in range(num_in):
        for e in range(local_experts):
            in_at[i, e] = at
            pieces.append((at, ins[i][1] // unit, i, e))
            at += ins[i][1] // unit
    out_units = local_experts * d_expert // unit_rows
    for n in range(num_out):
        out_at[n] = at
        pieces.append((at, out_units, None, n))
        at += out_units
    started = [0]

    def in_rows(i, e, w, t):
        first = (in_at[i, e] % RING) * unit_rows + (w * tiles + t) * ins[i][1]
        return slice(first, first + ins[i][1])

    def out_rows(n, e):
        first = (out_at[n] % RING) * unit_rows + e * d_expert
        return slice(first, first + d_expert)

    def in_group(i, lo):
        return i * (local_experts // EXP_GROUP) + lo // EXP_GROUP

    def fill(used):
        while started[0] < len(pieces):
            at, units, i, k = pieces[started[0]]
            if at + units > used + RING:
                break
            if i is None:
                for e in range(local_experts):
                    pltpu.make_async_copy(
                        w_two.at[e, :, pl.ds(*outs[k])],
                        pool.at[out_rows(k, e), 0 : outs[k][1]], out_sem.at[k],
                    ).start()
            else:
                for w, ref in enumerate((w_one, w_three)):
                    for t in range(tiles):
                        pltpu.make_async_copy(
                            ref.at[k, pl.ds(*ins[i]), pl.ds(t * COLS, COLS)],
                            pool.at[in_rows(i, k, w, t), :], in_sem.at[in_group(i, k)],
                        ).start()
            started[0] += 1

    def in_wait(i, lo):
        first = (in_at[i, lo] % RING) * unit_rows
        ref = pool.at[first : first + EXP_GROUP * 2 * tiles * ins[i][1], :]
        pltpu.make_async_copy(ref, ref, in_sem.at[in_group(i, lo)]).wait()

    def out_wait(n):
        first = (out_at[n] % RING) * unit_rows
        ref = pool.at[first : first + local_experts * d_expert, 0 : outs[n][1]]
        pltpu.make_async_copy(ref, ref, out_sem.at[n]).wait()

    def tok_copy():
        return pltpu.make_async_copy(tokens, xs.at[me], tok_sem)

    tok_copy().start()

    barrier = pltpu.get_barrier_semaphore()
    for k in range(1, num_dev):
        pl.semaphore_signal(
            barrier, inc=1, device_id={"ep": lax.rem(me + k, num_dev)}, device_id_type=MESH
        )

    expert_id = lax.broadcasted_iota(jnp.int32, (num_experts, num_tokens), 0)
    member = jnp.zeros((num_experts, num_tokens), F32)
    for j in range(top_k):
        member = member + jnp.where(routes[j : j + 1, :] == expert_id, 1.0, 0.0)
    row_id = lax.broadcasted_iota(jnp.int32, (num_tokens, num_tokens), 0)
    col_id = lax.broadcasted_iota(jnp.int32, (num_tokens, num_tokens), 1)
    before = jnp.where(row_id < col_id, 1.0, 0.0).astype(BF16)
    rank = jnp.dot(member.astype(BF16), before, preferred_element_type=F32)
    slot_of = jnp.where(member > 0.5, rank, -1.0)
    s_loc[...] = slot_of.reshape(num_dev, local_experts, num_tokens)
    s_all[me] = s_loc[me]

    with jax.named_scope("tok_wait"):
        tok_copy().wait()
    fill(0)

    with jax.named_scope("barrier"):
        pl.semaphore_wait(barrier, num_dev - 1)

    def plan_copy(k, src, dst, send, recv):
        peer = lax.rem(me + k, num_dev)
        return pltpu.make_async_remote_copy(
            src_ref=src.at[peer], dst_ref=dst.at[me], send_sem=send, recv_sem=recv,
            device_id={"ep": peer}, device_id_type=MESH,
        )

    def plan_all(src, dst, send, recv):
        return pltpu.make_async_remote_copy(
            src_ref=src.at[0 : num_dev - 1], dst_ref=dst.at[0 : num_dev - 1], send_sem=send,
            recv_sem=recv, device_id={"ep": partner}, device_id_type=MESH,
        )

    for k in range(1, num_dev):
        plan_copy(k, s_loc, s_all, s_send, s_recv).start()

    low, high, full = pl.ds(0, half), pl.ds(half, half), pl.ds(0, num_tokens)
    ag_table = (
        (me, full, right), (me, full, left), (me, full, partner),
        (left, low, right), (right, high, left),
        (left, full, partner), (right, full, partner),
        (opp, low, partner), (opp, high, partner),
    )

    ag_sem = (0, 1, 4, 2, 3, 4, 4, 4, 4)

    def ag(i, kind):
        block, rng, dest = ag_table[kind]
        ref = xs.at[block, rng, pl.ds(*ins[i])]
        return pltpu.make_async_remote_copy(
            src_ref=ref, dst_ref=ref, send_sem=ag_send,
            recv_sem=ag_recv.at[i, ag_sem[kind]], device_id={"ep": dest}, device_id_type=MESH,
        )

    def ag_partner(i):
        ref = xs.at[0 : num_dev // 2, :, pl.ds(*ins[i])]
        return pltpu.make_async_remote_copy(
            src_ref=ref, dst_ref=ref, send_sem=ag_send,
            recv_sem=ag_recv.at[i, 4], device_id={"ep": partner}, device_id_type=MESH,
        )

    def ag_own(i):
        if i < num_in:
            for kind in (0, 1, 2):
                ag(i, kind).start()

    def ag_stage1(i):
        if i < num_in:
            ag(i, 0).wait_recv()
            ag(i, 3).start()
            ag(i, 5).start()
            ag(i, 1).wait_recv()
            ag(i, 4).start()
            ag(i, 6).start()
            ag_own(i + 2)

    def ag_stage2(i):
        if i < num_in:
            ag(i, 3).wait_recv()
            ag(i, 7).start()
            ag(i, 4).wait_recv()
            ag(i, 8).start()

    def ag_stage3(i):
        if i < num_in:
            ag_partner(i).wait_recv()

    ag_own(0)

    def span(i):
        return ins[i][0], ins[i][0] + ins[i][1]

    dims = (((1,), (1,)), ((), ()))
    logits = jnp.zeros((num_experts, num_tokens), F32)
    for i in range(num_in):
        logits = logits + lax.dot_general(
            w_router[:, slice(*span(i))], xs[me, :, slice(*span(i))], dims, preferred_element_type=F32
        )
    chosen = member > 0.5
    peak = jnp.max(jnp.where(chosen, logits, -jnp.inf), axis=0, keepdims=True)
    powers = jnp.where(chosen, jnp.exp(jnp.where(chosen, logits - peak, 0.0)), 0.0)
    gates = powers / jnp.sum(powers, axis=0, keepdims=True)
    g_loc[...] = gates.reshape(num_dev, local_experts, num_tokens)
    g_all[me] = g_loc[me]
    for k in range(1, num_dev):
        plan_copy(k, g_loc, g_all, g_send, g_recv).start()
    ag_own(1)

    slot_id = lax.broadcasted_iota(jnp.int32, (cap, num_tokens), 0).astype(F32)
    with jax.named_scope("s_wait"):
        plan_all(s_loc, s_all, s_send, s_recv).wait_recv()

    def build_pick(q, carry):
        parts = [
            jnp.where(s_all[q, e : e + 1, :] == slot_id, 1.0, 0.0) for e in range(local_experts)
        ]
        pick[q] = jnp.concatenate(parts, axis=0).astype(BF16)
        return carry

    with jax.named_scope("build_pick"):
        lax.fori_loop(0, num_dev, build_pick, 0)

    def build_gates(q, carry):
        parts = [
            jnp.where(s_all[q, e : e + 1, :] == slot_id, g_all[q, e : e + 1, :], 0.0)
            for e in range(local_experts)
        ]
        mat = jnp.concatenate(parts, axis=0).T
        top = mat.astype(BF16)
        rest = mat - top.astype(F32)
        mid = rest.astype(BF16)
        gate_mat[q, 0:num_tokens] = top
        gate_mat[q, num_tokens : 2 * num_tokens] = mid
        gate_mat[q, 2 * num_tokens :] = (rest - mid.astype(F32)).astype(BF16)
        return carry

    def gather(i):
        def one_source(q):
            width = ins[i][1]
            picked = jnp.dot(pick[q], xs[q, :, slice(*span(i))], preferred_element_type=F32)
            us[:, pl.ds(q * cap, cap), 0:width] = picked.reshape(local_experts, cap, width)

        loop(num_dev, one_source, GATHER_UNROLL)

    def experts(i, first, last):
        for lo in range(first, last, EXP_GROUP):
            expert_group(i, lo, lo + EXP_GROUP)

    def expert_group(i, lo, hi):
        in_wait(i, lo)
        for e in range(lo, hi):
            u = us[e, :, 0 : ins[i][1]].astype(BF16)
            for t in range(tiles):
                cols = slice(t * COLS, (t + 1) * COLS)
                a = jnp.dot(u, pool[in_rows(i, e, 0, t), :], preferred_element_type=F32)
                b = jnp.dot(u, pool[in_rows(i, e, 1, t), :], preferred_element_type=F32)
                if i > 0:
                    a = a + acc_a[e, :, cols]
                    b = b + acc_b[e, :, cols]
                if i < num_in - 1:
                    acc_a[e, :, cols] = a
                    acc_b[e, :, cols] = b
                else:
                    hid[e, :, cols] = (jax.nn.silu(a) * b).astype(BF16)
        fill(in_at[i, hi - 1] + ins[i][1] // unit)

    with jax.named_scope("ag1_0"):
        ag_stage1(0)
    with jax.named_scope("g_wait"):
        plan_all(g_loc, g_all, g_send, g_recv).wait_recv()
    with jax.named_scope("build_gates"):
        lax.fori_loop(0, num_dev, build_gates, 0)
    with jax.named_scope("ag2_0"):
        ag_stage2(0)
    with jax.named_scope("ag1_1"):
        ag_stage1(1)
    with jax.named_scope("ag3_0"):
        ag_stage3(0)
    mid_expert = local_experts // 2
    for i in range(num_in):
        with jax.named_scope(f"gather_{i}"):
            gather(i)
        with jax.named_scope(f"experts_{i}a"):
            experts(i, 0, mid_expert)
        with jax.named_scope(f"ag1_{i + 2}"):
            ag_stage1(i + 2)
        with jax.named_scope(f"ag2_{i + 1}"):
            ag_stage2(i + 1)
        with jax.named_scope(f"experts_{i}b"):
            experts(i, mid_expert, local_experts)
        with jax.named_scope(f"ag3_{i + 1}"):
            ag_stage3(i + 1)

    def partial(n, q):
        nw = outs[n][1]
        base = pl.multiple_of(q * cap, 8)
        o_rows = us[:, pl.ds(base, cap), 0:nw].reshape(slots, nw).astype(BF16)
        total = jnp.dot(gate_mat[q], o_rows, preferred_element_type=F32)
        total = total.reshape(3, num_tokens, nw)
        return (total[2] + total[1]) + total[0]

    def width(n):
        return pl.ds(0, outs[n][1])

    order = (2, 1, 3, 0)

    def p_copy(n, part):
        js = slice(0, 1) if part == 0 else slice(1, num_chips)
        return pltpu.make_async_remote_copy(
            src_ref=p_send.at[n % 2, js, :, width(n)], dst_ref=p_recv.at[n, js, :, width(n)],
            send_sem=ps_sem.at[n % 2], recv_sem=pr_sem.at[n, part],
            device_id={"ep": partner}, device_id_type=MESH,
        )

    def p_sent(n):
        pltpu.make_async_remote_copy(
            src_ref=p_send.at[n % 2, :, :, width(n)], dst_ref=p_recv.at[n, :, :, width(n)],
            send_sem=ps_sem.at[n % 2], recv_sem=pr_sem.at[n, 0],
            device_id={"ep": partner}, device_id_type=MESH,
        ).wait_send()

    def h_copy(n, d):
        return pltpu.make_async_remote_copy(
            src_ref=own.at[n % OWN_SLOTS, 2, low if d == 0 else high, width(n)],
            dst_ref=h_recv.at[n, d, :, width(n)], send_sem=rs_send.at[n % OWN_SLOTS],
            recv_sem=hr_sem.at[n, d],
            device_id={"ep": right if d == 0 else left}, device_id_type=MESH,
        )

    def f_copy(n, d):
        return pltpu.make_async_remote_copy(
            src_ref=own.at[n % OWN_SLOTS, 1 if d == 0 else 3, :, width(n)],
            dst_ref=f_recv.at[n, d, :, width(n)], send_sem=rs_send.at[n % OWN_SLOTS],
            recv_sem=fr_sem.at[n],
            device_id={"ep": right if d == 0 else left}, device_id_type=MESH,
        )

    def ring_sent(n):
        ref = own.at[n % OWN_SLOTS, 0:3, :, width(n)]
        pltpu.make_async_remote_copy(
            src_ref=ref, dst_ref=ref, send_sem=rs_send.at[n % OWN_SLOTS], recv_sem=fr_sem.at[n],
            device_id={"ep": right}, device_id_type=MESH,
        ).wait_send()

    def down(n):
        out_wait(n)
        w = slice(0, outs[n][1])
        for e in range(local_experts):
            us[e, :, w] = jnp.dot(hid[e], pool[out_rows(n, e), w], preferred_element_type=F32)

    def combine(n):
        w = slice(0, outs[n][1])
        if n >= 2:
            p_sent(n - 2)
        if n >= OWN_SLOTS:
            ring_sent(n - OWN_SLOTS)
        for js in ((0,), (1, 2, 3)):
            for j in js:
                p_send[n % 2, j, :, w] = partial(n, at_chip(order[j]) * 2 + 1 - core)
            p_copy(n, js[0]).start() if js[0] == 0 else p_copy(n, 1).start()
            for j in js:
                own[n % OWN_SLOTS, order[j], :, w] = partial(n, at_chip(order[j]) * 2 + core)
        fill(out_at[n] + out_units)

    def send_halves(n):
        s, w = n % OWN_SLOTS, slice(0, outs[n][1])
        p_copy(n, 0).wait_recv()
        own[s, 2, :, w] = own[s, 2, :, w] + p_recv[n, 0, :, w]
        for d in (0, 1):
            h_copy(n, d).start()

    def add_partner(n):
        s, w = n % OWN_SLOTS, slice(0, outs[n][1])
        p_copy(n, 1).wait_recv()
        for j in (1, 2, 3):
            own[s, order[j], :, w] = own[s, order[j], :, w] + p_recv[n, j, :, w]

    def send_full(n):
        s, w = n % OWN_SLOTS, slice(0, outs[n][1])
        for d, k, rng in ((0, 1, low), (1, 3, high)):
            h_copy(n, d).wait_recv()
            own[s, k, rng, w] = own[s, k, rng, w] + h_recv[n, d, :, w]
            f_copy(n, d).start()

    def y_copy(n):
        cols = pl.ds(*outs[n])
        return pltpu.make_async_copy(y_buf.at[:, cols], out.at[:, cols], y_sem)

    def finish(n):
        s, w = n % OWN_SLOTS, slice(0, outs[n][1])
        ref = f_recv.at[n, :, :, width(n)]
        pltpu.make_async_remote_copy(
            src_ref=ref, dst_ref=ref, send_sem=rs_send.at[s], recv_sem=fr_sem.at[n],
            device_id={"ep": right}, device_id_type=MESH,
        ).wait_recv()
        y_buf[:, pl.ds(*outs[n])] = (
            own[s, 0, :, w] + (f_recv[n, 0, :, w] + f_recv[n, 1, :, w])
        ).astype(BF16)
        y_copy(n).start()

    def run(name, body, n, lag=0):
        if 0 <= n - lag < num_out:
            with jax.named_scope(f"{name}_{n - lag}"):
                body(n - lag)

    for n in range(num_out + FIN_LAG):
        run("down", down, n)
        if n >= 2:
            run("halves", send_halves, n, 1)
        run("combine", combine, n)
        if n == 0:
            run("halves", send_halves, n)
        run("add", add_partner, n, 1)
        run("full", send_full, n, 2)
        run("finish", finish, n, FIN_LAG)

    with jax.named_scope("end_plan"):
        plan_all(s_loc, s_all, s_send, s_recv).wait_send()
        plan_all(g_loc, g_all, g_send, g_recv).wait_send()
        sent = xs.at[0 : num_dev - 1]
        pltpu.make_async_remote_copy(
            src_ref=sent, dst_ref=sent, send_sem=ag_send, recv_sem=ag_recv.at[0, 4],
            device_id={"ep": partner}, device_id_type=MESH,
        ).wait_send()
    with jax.named_scope("end_ring"):
        for n in range(num_out - 2, num_out):
            p_sent(n)
        for n in range(num_out - OWN_SLOTS, num_out):
            ring_sent(n)
    with jax.named_scope("end_y"):
        pltpu.make_async_copy(y_buf, out, y_sem).wait()


def solution(mesh):
    num_dev = mesh.shape["ep"]
    row_spec = P(("dp", "ep"), None)
    expert_spec = P("ep", None, None)

    def device_step(tokens, routes, w_router, w_one, w_three, w_two):
        num_tokens, d_model = tokens.shape
        num_experts = w_router.shape[1]
        local_experts, _, d_expert = w_one.shape
        cap = slot_capacity(num_tokens, routes.shape[1], num_experts)
        rows, slots = num_dev * cap, local_experts * cap
        num_in, num_out = len(IN_SPLIT), len(OUT_SPLIT)
        unit = d_model // sum(IN_SPLIT)
        kc = unit * max(IN_SPLIT)
        nw = d_model // sum(OUT_SPLIT) * max(OUT_SPLIT)
        chips, half = num_dev // 2, num_tokens // 2
        dma = pltpu.SemaphoreType.DMA
        any_spec = pl.BlockSpec(memory_space=pl.ANY)
        vmem_spec = pl.BlockSpec(memory_space=pltpu.VMEM)
        return pl.pallas_call(
            functools.partial(moe_kernel, cap),
            out_shape=jax.ShapeDtypeStruct((num_tokens, d_model), BF16),
            in_specs=[any_spec, vmem_spec, vmem_spec, any_spec, any_spec, any_spec],
            out_specs=any_spec,
            scratch_shapes=[
                pltpu.VMEM((num_dev, num_tokens, d_model), BF16),
                pltpu.VMEM((local_experts, rows, kc), F32),
                pltpu.VMEM((local_experts, rows, d_expert), F32),
                pltpu.VMEM((local_experts, rows, d_expert), F32),
                pltpu.VMEM((local_experts, rows, d_expert), BF16),
                pltpu.VMEM((RING * 2 * d_expert // COLS * unit, COLS), BF16),
                pltpu.VMEM((num_tokens, d_model), BF16),
                pltpu.VMEM((num_dev, slots, num_tokens), BF16),
                pltpu.VMEM((num_dev, 3 * num_tokens, slots), BF16),
                pltpu.VMEM((num_dev, local_experts, num_tokens), F32),
                pltpu.VMEM((num_dev, local_experts, num_tokens), F32),
                pltpu.VMEM((num_dev, local_experts, num_tokens), F32),
                pltpu.VMEM((num_dev, local_experts, num_tokens), F32),
                pltpu.VMEM((OWN_SLOTS, chips, num_tokens, nw), F32),
                pltpu.VMEM((2, chips, num_tokens, nw), F32),
                pltpu.VMEM((num_out, chips, num_tokens, nw), F32),
                pltpu.VMEM((num_out, 2, half, nw), F32),
                pltpu.VMEM((num_out, 2, num_tokens, nw), F32),
                dma, dma((num_in * local_experts // EXP_GROUP,)), dma((num_out,)),
                dma, dma((num_in, 5)), dma, dma, dma, dma,
                dma((2,)), dma((num_out, 2)), dma((OWN_SLOTS,)), dma((num_out, 2)), dma((num_out,)), dma,
            ],
            compiler_params=pltpu.CompilerParams(
                collective_id=0, has_side_effects=True, vmem_limit_bytes=67_000_000
            ),
            name="moe_step",
        )(tokens, routes.T, w_router.T, w_one, w_three, w_two)

    return jax.shard_map(
        device_step, mesh=mesh,
        in_specs=(row_spec, row_spec, P(None, None), expert_spec, expert_spec, expert_spec),
        out_specs=row_spec, check_vma=False,
    )
```

time: 260 us -> 79.8 us (0.31)
  Pallas kernels: 0 us -> 77.5 us
  blocking collectives: 77.3 us -> 0 us
  other arithmetic: 60.2 us -> 0 us
  local copies, waits for them, and re-layouts: 51.1 us -> 1.88 us
  matrix products: 48.9 us -> 0 us
  waiting for transfers between devices: 16 us -> 0 us
  starting transfers between devices: 5.23 us -> 0 us
    pallas_call x0 -> x1, Pallas kernels: none -> 77.5 us  [device_step(): pl.pallas_call(functools.partial(moe_kernel, cap), out_shape=jax.ShapeDty...]
    all_to_all x1 -> x0, blocking collectives: 77.3 us -> none  [device_step(): recv_rows = lax.all_to_all(send_rows, 'ep', 0, 1, tiled=True)]
    dot_general x3 -> x0, matrix products: 48.9 us -> none  [the longest x1 30.3 us: expert_mlp(): jnp.einsum('erf,efd->erd', hidden, w_two, preferred_element_type=jnp.floa...]
    gather x6 -> x0, other arithmetic: 40.5 us -> none  [the longest x1 35.3 us: device_step(): back_rows.reshape(num_experts * capacity, d_model)[pair_row]]
    gather x13 -> x0, local copies, waits for them, and re-layouts: 35.6 us -> none  [the longest x1 12.4 us: device_step(): back_rows.reshape(num_experts * capacity, d_model)[pair_row]]
    all_to_all x1 -> x0, waiting for transfers between devices: 16 us -> none  [device_step(): lax.all_to_all(out_rows.reshape(local_experts, group_size, capacity, d_mo...]
    scatter-add x1 -> x0, other arithmetic: 7.61 us -> none  [dispatch_plan(): jax.ops.segment_sum(jnp.ones_like(flat_routes), flat_routes, num_segments...]
    reduce_sum x2 -> x0, other arithmetic: 7.35 us -> none  [the longest x1 7.33 us: device_step(): jnp.sum(gate_vals[:, :, None] * pair_out, axis=1).astype(jnp.bfloat16)]
  transfers between devices with their start and end apart: 1 -> 0, of which waited for: 1 -> 0; matrix products, arithmetic and copies ran while one was open for 21% -> 0% of each run, Pallas kernels for 0% -> 0%
where the time goes in v2:
time: 79.8 us; the launch traced here: 79.4 us
  Pallas kernels  77.5 us (97%)
  local copies, waits for them, and re-layouts  1.88 us (2%)
    pallas_call x1, Pallas kernels, device_step(): pl.pallas_call(functools.partial(moe_kernel, cap), out_shape=jax.ShapeDty...  77.5 us
    unnamed x1, local copies, waits for them, and re-layouts  1.88 us

profile of v2, /device:TPU:112, one launch (start us, length us, event | category | flops | bytes accessed | tf_op | source)
XLA Modules:
  0.0 79.4 jit_solution(15553321015428316555)
XLA Ops:
  0.0 77.5 %moe_step.1 = bf16[128,2048]{1,0:T(8,128)(2,1)} custom-call(bf16[128,2048]{1,0:T(8,128)(2,1)} %tokens.1, s32[8,128]{1,0:T(8,128)} %bitcast.3, bf16[64,2048]{1,0:T(8,128)(2,1)} %bitcast.2, bf16[8,2048,1024]{2,1,0:T(8,128)(2,1)} %w_one.1, bf16[8,2048,1024]{2,1,0:T(8,128)(2,1)} %w_three.1, bf16[8,1024,2048]{2,1,0:T(8,128)(2,1)} %w_two.1), custom_call_target="tpu_custom_call" | custom-call | tf_op jit(solution)/shard_map/moe_step/pallas_call | solution.py:503
  77.5 1.9 %copy.8 = bf16[128,2048]{1,0:T(8,128)(2,1)} copy(bf16[128,2048]{1,0:T(8,128)(2,1)} %moe_step.1) | data formatting | bytes 1048576

commit v3 on v2

--- a/solution.py
+++ b/solution.py
@@ -12,13 +12,17 @@
 BF16 = jnp.bfloat16
 
 IN_SPLIT = (1, 2, 2, 2, 1)
+AG_START = ("s", "f0", "o2", "g", "f1", "o3", "h0", "p0")
+AG_PLAN = (((), (), ("f2", "h1", "p1")), (("o4",), ("f3", "h2"), ("p2",)), ((), ("f4", "h3"), ("p3",)), ((), ("h4",), ("p4",)), ((), (), ()))
 OUT_SPLIT = (2, 2, 2, 2, 2, 2, 2, 2)
 RING = 24
 OWN_SLOTS = 4
 FIN_LAG = 3
+EARLY = 2
+FULL_EARLY = 1
 COLS = 256
 EXP_GROUP = 4
-GATHER_UNROLL = 4
+GATHER_UNROLL = 8
 
 
 def chunk_list(parts, total):
@@ -49,11 +53,11 @@
 
 
 def moe_kernel(
-    cap, tokens, routes, w_router, w_one, w_three, w_two, out,
-    xs, us, acc_a, acc_b, hid, pool, y_buf, pick, gate_mat,
+    cap, tokens, routes_in, w_router_in, w_one, w_three, w_two, out,
+    routes, w_router, xs, us, acc_a, acc_b, hid, pool, pick, gate_mat,
     s_loc, g_loc, s_all, g_all, own, p_send, p_recv, h_recv, f_recv,
-    tok_sem, in_sem, out_sem, ag_send, ag_recv, s_send, s_recv, g_send, g_recv,
-    ps_sem, pr_sem, rs_send, hr_sem, fr_sem, y_sem,
+    tok_sem, route_sem, router_sem, in_sem, out_sem, ag_send, ag_recv, s_send, s_recv, g_send, g_recv,
+    ps_sem, pr_sem, rs_send, hr_sem, fr_sem,
 ):
     num_tokens, d_model = tokens.shape
     top_k = routes.shape[0]
@@ -141,7 +145,11 @@
     def tok_copy():
         return pltpu.make_async_copy(tokens, xs.at[me], tok_sem)
 
+    route_copy = pltpu.make_async_copy(routes_in, routes, route_sem)
+    router_copy = pltpu.make_async_copy(w_router_in, w_router, router_sem)
     tok_copy().start()
+    route_copy.start()
+    router_copy.start()
 
     barrier = pltpu.get_barrier_semaphore()
     for k in range(1, num_dev):
@@ -149,6 +157,66 @@
             barrier, inc=1, device_id={"ep": lax.rem(me + k, num_dev)}, device_id_type=MESH
         )
 
+    with jax.named_scope("tok_wait"):
+        tok_copy().wait()
+    fill(0)
+
+    with jax.named_scope("barrier"):
+        pl.semaphore_wait(barrier, num_dev - 1)
+
+    low, high, full = pl.ds(0, half), pl.ds(half, half), pl.ds(0, num_tokens)
+    ag_table = (
+        (me, full, right), (me, full, left), (me, full, partner),
+        (left, low, right), (right, high, left),
+        (left, full, partner), (right, full, partner),
+        (opp, low, partner), (opp, high, partner),
+    )
+
+    ag_sem = (0, 1, 4, 2, 3, 4, 4, 4, 4)
+
+    def ag(i, kind):
+        block, rng, dest = ag_table[kind]
+        ref = xs.at[block, rng, pl.ds(*ins[i])]
+        return pltpu.make_async_remote_copy(
+            src_ref=ref, dst_ref=ref, send_sem=ag_send,
+            recv_sem=ag_recv.at[i, ag_sem[kind]], device_id={"ep": dest}, device_id_type=MESH,
+        )
+
+    def ag_partner(i):
+        ref = xs.at[0 : num_dev // 2, :, pl.ds(*ins[i])]
+        return pltpu.make_async_remote_copy(
+            src_ref=ref, dst_ref=ref, send_sem=ag_send,
+            recv_sem=ag_recv.at[i, 4], device_id={"ep": partner}, device_id_type=MESH,
+        )
+
+    def ag_own(i):
+        if i < num_in:
+            for kind in (0, 1, 2):
+                ag(i, kind).start()
+
+    def ag_stage1(i):
+        if i < num_in:
+            ag(i, 0).wait_recv()
+            ag(i, 3).start()
+            ag(i, 5).start()
+            ag(i, 1).wait_recv()
+            ag(i, 4).start()
+            ag(i, 6).start()
+
+    def ag_stage2(i):
+        if i < num_in:
+            ag(i, 3).wait_recv()
+            ag(i, 7).start()
+            ag(i, 4).wait_recv()
+            ag(i, 8).start()
+
+    def ag_stage3(i):
+        if i < num_in:
+            ag_partner(i).wait_recv()
+
+    ag_own(0)
+
+    route_copy.wait()
     expert_id = lax.broadcasted_iota(jnp.int32, (num_experts, num_tokens), 0)
     member = jnp.zeros((num_experts, num_tokens), F32)
     for j in range(top_k):
@@ -161,13 +229,6 @@
     s_loc[...] = slot_of.reshape(num_dev, local_experts, num_tokens)
     s_all[me] = s_loc[me]
 
-    with jax.named_scope("tok_wait"):
-        tok_copy().wait()
-    fill(0)
-
-    with jax.named_scope("barrier"):
-        pl.semaphore_wait(barrier, num_dev - 1)
-
     def plan_copy(k, src, dst, send, recv):
         peer = lax.rem(me + k, num_dev)
         return pltpu.make_async_remote_copy(
@@ -184,64 +245,12 @@
     for k in range(1, num_dev):
         plan_copy(k, s_loc, s_all, s_send, s_recv).start()
 
-    low, high, full = pl.ds(0, half), pl.ds(half, half), pl.ds(0, num_tokens)
-    ag_table = (
-        (me, full, right), (me, full, left), (me, full, partner),
-        (left, low, right), (right, high, left),
-        (left, full, partner), (right, full, partner),
-        (opp, low, partner), (opp, high, partner),
-    )
-
-    ag_sem = (0, 1, 4, 2, 3, 4, 4, 4, 4)
-
-    def ag(i, kind):
-        block, rng, dest = ag_table[kind]
-        ref = xs.at[block, rng, pl.ds(*ins[i])]
-        return pltpu.make_async_remote_copy(
-            src_ref=ref, dst_ref=ref, send_sem=ag_send,
-            recv_sem=ag_recv.at[i, ag_sem[kind]], device_id={"ep": dest}, device_id_type=MESH,
-        )
-
-    def ag_partner(i):
-        ref = xs.at[0 : num_dev // 2, :, pl.ds(*ins[i])]
-        return pltpu.make_async_remote_copy(
-            src_ref=ref, dst_ref=ref, send_sem=ag_send,
-            recv_sem=ag_recv.at[i, 4], device_id={"ep": partner}, device_id_type=MESH,
-        )
-
-    def ag_own(i):
-        if i < num_in:
-            for kind in (0, 1, 2):
-                ag(i, kind).start()
-
-    def ag_stage1(i):
-        if i < num_in:
-            ag(i, 0).wait_recv()
-            ag(i, 3).start()
-            ag(i, 5).start()
-            ag(i, 1).wait_recv()
-            ag(i, 4).start()
-            ag(i, 6).start()
-            ag_own(i + 2)
-
-    def ag_stage2(i):
-        if i < num_in:
-            ag(i, 3).wait_recv()
-            ag(i, 7).start()
-            ag(i, 4).wait_recv()
-            ag(i, 8).start()
-
-    def ag_stage3(i):
-        if i < num_in:
-            ag_partner(i).wait_recv()
-
-    ag_own(0)
-
     def span(i):
         return ins[i][0], ins[i][0] + ins[i][1]
 
     dims = (((1,), (1,)), ((), ()))
     logits = jnp.zeros((num_experts, num_tokens), F32)
+    router_copy.wait()
     for i in range(num_in):
         logits = logits + lax.dot_general(
             w_router[:, slice(*span(i))], xs[me, :, slice(*span(i))], dims, preferred_element_type=F32
@@ -257,9 +266,6 @@
     ag_own(1)
 
     slot_id = lax.broadcasted_iota(jnp.int32, (cap, num_tokens), 0).astype(F32)
-    with jax.named_scope("s_wait"):
-        plan_all(s_loc, s_all, s_send, s_recv).wait_recv()
-
     def build_pick(q, carry):
         parts = [
             jnp.where(s_all[q, e : e + 1, :] == slot_id, 1.0, 0.0) for e in range(local_experts)
@@ -267,8 +273,6 @@
         pick[q] = jnp.concatenate(parts, axis=0).astype(BF16)
         return carry
 
-    with jax.named_scope("build_pick"):
-        lax.fori_loop(0, num_dev, build_pick, 0)
 
     def build_gates(q, carry):
         parts = [
@@ -290,7 +294,13 @@
             picked = jnp.dot(pick[q], xs[q, :, slice(*span(i))], preferred_element_type=F32)
             us[:, pl.ds(q * cap, cap), 0:width] = picked.reshape(local_experts, cap, width)
 
-        loop(num_dev, one_source, GATHER_UNROLL)
+        if GATHER_UNROLL < num_dev:
+            loop(num_dev, one_source, GATHER_UNROLL)
+        else:
+
+            @pl.when(me >= 0)
+            def _():
+                loop(num_dev, one_source, num_dev)
 
     def experts(i, first, last):
         for lo in range(first, last, EXP_GROUP):
@@ -314,32 +324,34 @@
                     hid[e, :, cols] = (jax.nn.silu(a) * b).astype(BF16)
         fill(in_at[i, hi - 1] + ins[i][1] // unit)
 
-    with jax.named_scope("ag1_0"):
-        ag_stage1(0)
-    with jax.named_scope("g_wait"):
+    def slots_ready():
+        plan_all(s_loc, s_all, s_send, s_recv).wait_recv()
+        lax.fori_loop(0, num_dev, build_pick, 0)
+
+    def gates_ready():
         plan_all(g_loc, g_all, g_send, g_recv).wait_recv()
-    with jax.named_scope("build_gates"):
         lax.fori_loop(0, num_dev, build_gates, 0)
-    with jax.named_scope("ag2_0"):
-        ag_stage2(0)
-    with jax.named_scope("ag1_1"):
-        ag_stage1(1)
-    with jax.named_scope("ag3_0"):
-        ag_stage3(0)
+
+    plans = {"s": slots_ready, "g": gates_ready}
+    actions = {"f": ag_stage1, "h": ag_stage2, "p": ag_stage3, "o": ag_own}
+
+    def hook(items):
+        for item in items:
+            with jax.named_scope("ag_" + item):
+                actions[item[0]](int(item[1:])) if item[1:] else plans[item]()
+
+    hook(AG_START)
     mid_expert = local_experts // 2
     for i in range(num_in):
         with jax.named_scope(f"gather_{i}"):
             gather(i)
+        hook(AG_PLAN[i][0])
         with jax.named_scope(f"experts_{i}a"):
             experts(i, 0, mid_expert)
-        with jax.named_scope(f"ag1_{i + 2}"):
-            ag_stage1(i + 2)
-        with jax.named_scope(f"ag2_{i + 1}"):
-            ag_stage2(i + 1)
+        hook(AG_PLAN[i][1])
         with jax.named_scope(f"experts_{i}b"):
             experts(i, mid_expert, local_experts)
-        with jax.named_scope(f"ag3_{i + 1}"):
-            ag_stage3(i + 1)
+        hook(AG_PLAN[i][2])
 
     def partial(n, q):
         nw = outs[n][1]
@@ -404,12 +416,12 @@
             p_sent(n - 2)
         if n >= OWN_SLOTS:
             ring_sent(n - OWN_SLOTS)
-        for js in ((0,), (1, 2, 3)):
+        for part, js in enumerate(((0,), (1, 2, 3))):
             for j in js:
                 p_send[n % 2, j, :, w] = partial(n, at_chip(order[j]) * 2 + 1 - core)
-            p_copy(n, js[0]).start() if js[0] == 0 else p_copy(n, 1).start()
-            for j in js:
-                own[n % OWN_SLOTS, order[j], :, w] = partial(n, at_chip(order[j]) * 2 + core)
+            p_copy(n, part).start()
+        for j in range(num_chips):
+            own[n % OWN_SLOTS, order[j], :, w] = partial(n, at_chip(order[j]) * 2 + core)
         fill(out_at[n] + out_units)
 
     def send_halves(n):
@@ -431,10 +443,6 @@
             h_copy(n, d).wait_recv()
             own[s, k, rng, w] = own[s, k, rng, w] + h_recv[n, d, :, w]
             f_copy(n, d).start()
-
-    def y_copy(n):
-        cols = pl.ds(*outs[n])
-        return pltpu.make_async_copy(y_buf.at[:, cols], out.at[:, cols], y_sem)
 
     def finish(n):
         s, w = n % OWN_SLOTS, slice(0, outs[n][1])
@@ -443,10 +451,9 @@
             src_ref=ref, dst_ref=ref, send_sem=rs_send.at[s], recv_sem=fr_sem.at[n],
             device_id={"ep": right}, device_id_type=MESH,
         ).wait_recv()
-        y_buf[:, pl.ds(*outs[n])] = (
+        out[:, pl.ds(*outs[n])] = (
             own[s, 0, :, w] + (f_recv[n, 0, :, w] + f_recv[n, 1, :, w])
         ).astype(BF16)
-        y_copy(n).start()
 
     def run(name, body, n, lag=0):
         if 0 <= n - lag < num_out:
@@ -455,13 +462,17 @@
 
     for n in range(num_out + FIN_LAG):
         run("down", down, n)
-        if n >= 2:
+        if n >= 1 + EARLY:
             run("halves", send_halves, n, 1)
+        if FULL_EARLY:
+            run("add", add_partner, n, 2)
+            run("full", send_full, n, 2)
         run("combine", combine, n)
-        if n == 0:
+        if n < EARLY:
             run("halves", send_halves, n)
-        run("add", add_partner, n, 1)
-        run("full", send_full, n, 2)
+        if not FULL_EARLY:
+            run("add", add_partner, n, 1)
+            run("full", send_full, n, 2)
         run("finish", finish, n, FIN_LAG)
 
     with jax.named_scope("end_plan"):
@@ -477,8 +488,6 @@
             p_sent(n)
         for n in range(num_out - OWN_SLOTS, num_out):
             ring_sent(n)
-    with jax.named_scope("end_y"):
-        pltpu.make_async_copy(y_buf, out, y_sem).wait()
 
 
 def solution(mesh):
@@ -499,20 +508,20 @@
         chips, half = num_dev // 2, num_tokens // 2
         dma = pltpu.SemaphoreType.DMA
         any_spec = pl.BlockSpec(memory_space=pl.ANY)
-        vmem_spec = pl.BlockSpec(memory_space=pltpu.VMEM)
         return pl.pallas_call(
             functools.partial(moe_kernel, cap),
-            out_shape=jax.ShapeDtypeStruct((num_tokens, d_model), BF16),
-            in_specs=[any_spec, vmem_spec, vmem_spec, any_spec, any_spec, any_spec],
-            out_specs=any_spec,
+            out_shape=pltpu.VMEM((num_tokens, d_model), BF16),
+            in_specs=[any_spec] * 6,
+            out_specs=pl.BlockSpec(memory_space=pltpu.VMEM),
             scratch_shapes=[
+                pltpu.VMEM(routes.shape[::-1], jnp.int32),
+                pltpu.VMEM(w_router.shape[::-1], BF16),
                 pltpu.VMEM((num_dev, num_tokens, d_model), BF16),
                 pltpu.VMEM((local_experts, rows, kc), F32),
                 pltpu.VMEM((local_experts, rows, d_expert), F32),
                 pltpu.VMEM((local_experts, rows, d_expert), F32),
                 pltpu.VMEM((local_experts, rows, d_expert), BF16),
                 pltpu.VMEM((RING * 2 * d_expert // COLS * unit, COLS), BF16),
-                pltpu.VMEM((num_tokens, d_model), BF16),
                 pltpu.VMEM((num_dev, slots, num_tokens), BF16),
                 pltpu.VMEM((num_dev, 3 * num_tokens, slots), BF16),
                 pltpu.VMEM((num_dev, local_experts, num_tokens), F32),
@@ -524,12 +533,12 @@
                 pltpu.VMEM((num_out, chips, num_tokens, nw), F32),
                 pltpu.VMEM((num_out, 2, half, nw), F32),
                 pltpu.VMEM((num_out, 2, num_tokens, nw), F32),
-                dma, dma((num_in * local_experts // EXP_GROUP,)), dma((num_out,)),
+                dma, dma, dma, dma((num_in * local_experts // EXP_GROUP,)), dma((num_out,)),
                 dma, dma((num_in, 5)), dma, dma, dma, dma,
-                dma((2,)), dma((num_out, 2)), dma((OWN_SLOTS,)), dma((num_out, 2)), dma((num_out,)), dma,
+                dma((2,)), dma((num_out, 2)), dma((OWN_SLOTS,)), dma((num_out, 2)), dma((num_out,)),
             ],
             compiler_params=pltpu.CompilerParams(
-                collective_id=0, has_side_effects=True, vmem_limit_bytes=67_000_000
+                collective_id=0, has_side_effects=True, vmem_limit_bytes=65_000_000
             ),
             name="moe_step",
         )(tokens, routes.T, w_router.T, w_one, w_three, w_two)

time: 79.8 us -> 75 us (0.940)
  Pallas kernels: 77.5 us -> 74.1 us
  local copies, waits for them, and re-layouts: 1.88 us -> 0.8 us
    pallas_call x1, Pallas kernels: 77.5 us -> 74.1 us  [device_step(): pl.pallas_call(functools.partial(moe_kernel, cap), out_shape=pltpu.VMEM((...]
    unnamed x1, local copies, waits for them, and re-layouts: 1.88 us -> 0.8 us
where the time goes in v3:
time: 75 us; the launch traced here: 74.9 us
  Pallas kernels  74.1 us (99%)
  local copies, waits for them, and re-layouts  0.8 us (1%)
    pallas_call x1, Pallas kernels, device_step(): pl.pallas_call(functools.partial(moe_kernel, cap), out_shape=pltpu.VMEM((...  74.1 us

profile of v3, /device:TPU:112, one launch (start us, length us, event | category | flops | bytes accessed | tf_op | source)
XLA Modules:
  0.0 74.9 jit_solution(1744925578862559112)
XLA Ops:
  0.0 74.1 %moe_step.1 = bf16[128,2048]{1,0:T(8,128)(2,1)S(1)} custom-call(bf16[128,2048]{1,0:T(8,128)(2,1)} %tokens.1, s32[8,128]{1,0:T(8,128)} %bitcast.3, bf16[64,2048]{1,0:T(8,128)(2,1)} %bitcast.2, bf16[8,2048,1024]{2,1,0:T(8,128)(2,1)} %w_one.1, bf16[8,2048,1024]{2,1,0:T(8,128)(2,1)} %w_three.1, bf16[8,1024,2048]{2,1,0:T(8,128)(2,1)} %w_two.1), custom_call_target="tpu_custom_call" | custom-call | tf_op jit(solution)/shard_map/moe_step/pallas_call | solution.py:511
  74.1 0.8 %copy.8 = bf16[128,2048]{1,0:T(8,128)(2,1)} copy(bf16[128,2048]{1,0:T(8,128)(2,1)S(1)} %moe_step.1) | data formatting | bytes 1048576
